TPU v7x, 32 devices: a whole 2x2x4 slice. The times are simulated.
32 devices in a mesh: gx: 4 (over y, core), gy: 4 (over z), gz: 2 (over x).
Axes of the slice: x: 2, y: 2, z: 4, core: 2. Of those that a mesh axis runs over, the one named last changes fastest.
Arguments:
- residual: float32 [32, 128, 256], P('gx', 'gy', 'gz'), may hold values from -32 to 32
- direction: float32 [32, 128, 256], P('gx', 'gy', 'gz'), may hold values from -32 to 32
- diagonal: float32 [32, 128, 256], P('gx', 'gy', 'gz'), may hold values from 0.5 to 2
- recycled: bfloat16 [16, 32, 128, 256], P(None, 'gx', 'gy', 'gz'), may hold values from -6 to 6
- recycled_images: bfloat16 [16, 32, 128, 256], P(None, 'gx', 'gy', 'gz'), may hold values from -0.0014648438 to 0.0014648438
- coupling_inverse: float32 [16, 16], replicated, may hold values from -1 to 3, as said below
Outputs:
- solution_delta: float32 [32, 128, 256], P('gx', 'gy', 'gz')
- new_residual: float32 [32, 128, 256], P('gx', 'gy', 'gz')
- new_direction: float32 [32, 128, 256], P('gx', 'gy', 'gz')
Inputs may be any that keep to these rules, and one draw needn't show every extreme that they name: `coupling_inverse`: symmetric.
All inputs are finite; a program needn't handle non-finite values.
Results may differ from a plain program's by a relative error of at most 0.0028.
Values sent between devices are 32-bit elements; how exact they have to be, the bound alone decides.
No kernel may reach another device: no remote copies, remote signals or barrier semaphores. Data moves between devices by JAX's collectives and lax.ppermute only.
A program may use at most 64 MiB of HBM per device.

v0:
```python
import jax
import jax.numpy as jnp
import numpy as np
from jax import lax
from jax.sharding import PartitionSpec as P

S = 4
BASIS = 9
center = 7.25
half_width = 6.75


def extended(block, sides, width):
    for axis, dim in sides:
        count = lax.axis_size(axis)
        forward = [(i, i + 1) for i in range(count - 1)]
        forward.append((count - 1, 0))
        backward = [(target, source) for source, target in forward]
        low = lax.ppermute(
            lax.slice_in_dim(block, block.shape[dim] - width, None, axis=dim), axis, forward
        )
        high = lax.ppermute(lax.slice_in_dim(block, 0, width, axis=dim), axis, backward)
        block = jnp.concatenate([low, block, high], axis=dim)
    return block


def inside(padded):
    centre_cells = padded[:, 1:-1, 1:-1, 1:-1]
    beside_all = padded[:, 2:, 1:-1, 1:-1] + padded[:, :-2, 1:-1, 1:-1]
    beside_all = beside_all + padded[:, 1:-1, 2:, 1:-1] + padded[:, 1:-1, :-2, 1:-1]
    beside_all = beside_all + padded[:, 1:-1, 1:-1, 2:] + padded[:, 1:-1, 1:-1, :-2]
    return (centre_cells, beside_all)


def trim_margin(values, margin):
    if margin == 0:
        return values
    return values[..., margin:-margin, margin:-margin, margin:-margin]


def chebyshev_next(current, beside_all, diagonal, earlier):
    mapped = (6.0 + diagonal) * current - beside_all
    scaled = (mapped - center * current) / half_width
    if earlier is None:
        return scaled
    return 2.0 * scaled - earlier


def recurrence_matrix():
    recurrence = np.zeros((BASIS, BASIS), np.float32)
    for offset, length in ((0, S + 1), (S + 1, S)):
        recurrence[offset, offset] = center
        recurrence[offset + 1, offset] = half_width
        for column in range(1, length - 1):
            recurrence[offset + column + 1, offset + column] = half_width / 2
            recurrence[offset + column, offset + column] = center
            recurrence[offset + column - 1, offset + column] = half_width / 2
    return jnp.asarray(recurrence, dtype=jnp.float32)


def coordinates(totals, coupling_inverse):
    precise = lax.Precision.HIGHEST
    gram_block = totals[:BASIS]
    projections = totals[BASIS:]
    recurrence = recurrence_matrix()
    counter = jnp.arange(BASIS)
    residue = (counter == S + 1).astype(jnp.float32)
    search = (counter == 0).astype(jnp.float32)
    update = jnp.zeros((BASIS,), jnp.float32)
    norm_now = jnp.dot(residue, jnp.dot(gram_block, residue, precision=precise), precision=precise)
    for iteration in range(S):
        mapped = jnp.dot(recurrence, search, precision=precise)
        step_size = norm_now / jnp.dot(
            search, jnp.dot(gram_block, mapped, precision=precise), precision=precise
        )
        update = update + step_size * search
        residue = residue - step_size * mapped
        norm_next = jnp.dot(
            residue, jnp.dot(gram_block, residue, precision=precise), precision=precise
        )
        search = residue + norm_next / norm_now * search
        norm_now = norm_next
    weights = jnp.dot(
        coupling_inverse, jnp.dot(projections, residue, precision=precise), precision=precise
    )
    return (update, residue, search, weights.astype(jnp.bfloat16))


def body(residual, direction, diagonal, recycled, recycled_images, coupling_inverse):
    precise = lax.Precision.HIGHEST
    search_basis = [direction]
    residue_basis = [residual]
    earlier = None
    packed = jnp.stack([direction, residual, diagonal])
    padded = extended(packed, (("gx", 1), ("gy", 2), ("gz", 3)), S)
    wide_diag = padded[2]
    current = padded[:2]
    for iteration in range(S):
        if iteration == S - 1:
            current = current[:1]
            earlier = earlier[:1]
        centre_cells, beside_all = inside(current)
        margin = S - iteration - 1
        local_diag = trim_margin(wide_diag, iteration + 1)
        previous = None if earlier is None else trim_margin(earlier, 2)
        following = chebyshev_next(centre_cells, beside_all, local_diag, previous)
        earlier, current = (current, following)
        search_basis.append(trim_margin(following[0], margin))
        if following.shape[0] > 1:
            residue_basis.append(trim_margin(following[1], margin))
    basis = jnp.stack(search_basis + residue_basis)
    basis_flat = basis.reshape(basis.shape[0], -1)
    gram_block = lax.dot_general(
        basis_flat,
        basis_flat,
        (((1,), (1,)), ((), ())),
        precision=precise,
        preferred_element_type=jnp.float32,
    )
    rounded = basis_flat.astype(jnp.bfloat16)
    images = recycled_images.reshape(recycled_images.shape[0], -1)
    projections = lax.dot_general(
        images, rounded, (((1,), (1,)), ((), ())), preferred_element_type=jnp.float32
    )
    totals = lax.psum(jnp.concatenate([gram_block, projections], 0), ("gx", "gy", "gz"))
    update, residue, search, weights = coordinates(totals, coupling_inverse)
    shape = residual.shape
    solution_delta = jnp.dot(update, basis_flat, precision=precise).reshape(shape)
    new_residual = jnp.dot(residue, basis_flat, precision=precise).reshape(shape)
    correction = jnp.dot(
        weights, recycled.reshape(recycled.shape[0], -1), preferred_element_type=jnp.float32
    )
    new_direction = (jnp.dot(search, basis_flat, precision=precise) - correction).reshape(shape)
    return (solution_delta, new_residual, new_direction)


def solution(mesh):
    in_specs = (
        P("gx", "gy", "gz"),
        P("gx", "gy", "gz"),
        P("gx", "gy", "gz"),
        P(None, "gx", "gy", "gz"),
        P(None, "gx", "gy", "gz"),
        P(),
    )
    out_specs = (P("gx", "gy", "gz"), P("gx", "gy", "gz"), P("gx", "gy", "gz"))
    return jax.shard_map(body, mesh=mesh, in_specs=in_specs, out_specs=out_specs, check_vma=False)
```

profile of v0, /device:TPU:0, one launch (start us, length us, event | category | flops | bytes accessed | tf_op | source)
XLA Modules:
  0.0 110.9 jit_solution(13209403578807758797)
XLA Ops:
  0.7 1.1 %pad_maximum_fusion.2 = f32[3,8,32,128]{3,2,1,0:T(8,128)S(1)} fusion(f32[1,8,32,128]{3,2,1,0:T(8,128)} %bitcast.257, f32[1,8,32,128]{3,2,1,0:T(8,128)} %bitcast.251, f32[1,8,32,128]{3,2,1,0:T(8,128)} %bitcast.245), kind=kLoop, calls=%fused_computation.81 | loop fusion | flops 196608 | bytes 786432 | tf_op jit(solution)/shard_map/stack | solution.py:94
  1.8 0.5 collective-permute-start
  2.4 2.0 %collective-permute-start.1 = (f32[3,4,32,128]{3,2,1,0:T(8,128)S(1)}, f32[3,4,32,128]{3,2,1,0:T(8,128)S(1)}, u32[]{:S(2)}, u32[]{:S(2)}) collective-permute-start(f32[3,4,32,128]{3,2,1,0:T(8,128)S(1)} %get-tuple-element.14), channel_id=1, source_target_pairs={{8,0},{16,8},{24,16},{0,24},{9,1},{17,9},{25,17},{1,25},{10,2},{18... | collective-permute-start | bytes 589832 | tf_op jit(solution)/shard_map/ppermute | solution.py:22
  4.4 3.3 %collective-permute-done = f32[3,4,32,128]{3,2,1,0:T(8,128)S(1)} collective-permute-done((f32[3,4,32,128]{3,2,1,0:T(8,128)S(1)}, f32[3,4,32,128]{3,2,1,0:T(8,128)S(1)}, u32[]{:S(2)}, u32[]{:S(2)}) %collective-permute-start) | collective-permute-done | bytes 196640 | tf_op jit(solution)/shard_map/ppermute | solution.py:19
  7.7 1.9 %collective-permute-done.1 = f32[3,4,32,128]{3,2,1,0:T(8,128)S(1)} collective-permute-done((f32[3,4,32,128]{3,2,1,0:T(8,128)S(1)}, f32[3,4,32,128]{3,2,1,0:T(8,128)S(1)}, u32[]{:S(2)}, u32[]{:S(2)}) %collective-permute-start.1) | collective-permute-done | bytes 196640 | tf_op jit(solution)/shard_map/ppermute | solution.py:22
  9.6 0.9 pad_maximum_fusion.7
  10.5 1.6 %collective-permute-start.2 = (f32[3,16,4,128]{3,2,1,0:T(4,128)S(1)}, f32[3,16,4,128]{3,2,1,0:T(4,128)S(1)}, u32[]{:S(2)}, u32[]{:S(2)}) collective-permute-start(f32[3,16,4,128]{3,2,1,0:T(4,128)S(1)} %get-tuple-element.11), channel_id=1, source_target_pairs={{0,2},{2,4},{4,6},{6,0},{1,3},{3,5},{5,7},{7,1},{8,10},{10,12},{12... | collective-permute-start | bytes 294920 | tf_op jit(solution)/shard_map/ppermute | solution.py:19
  12.1 2.2 %collective-permute-start.3 = (f32[3,16,4,128]{3,2,1,0:T(4,128)S(1)}, f32[3,16,4,128]{3,2,1,0:T(4,128)S(1)}, u32[]{:S(2)}, u32[]{:S(2)}) collective-permute-start(f32[3,16,4,128]{3,2,1,0:T(4,128)S(1)} %get-tuple-element.12), channel_id=1, source_target_pairs={{2,0},{4,2},{6,4},{0,6},{3,1},{5,3},{7,5},{1,7},{10,8},{12,10},{14... | collective-permute-start | bytes 294920 | tf_op jit(solution)/shard_map/ppermute | solution.py:22
  14.4 3.7 %collective-permute-done.2 = f32[3,16,4,128]{3,2,1,0:T(4,128)S(1)} collective-permute-done((f32[3,16,4,128]{3,2,1,0:T(4,128)S(1)}, f32[3,16,4,128]{3,2,1,0:T(4,128)S(1)}, u32[]{:S(2)}, u32[]{:S(2)}) %collective-permute-start.2) | collective-permute-done | bytes 98336 | tf_op jit(solution)/shard_map/ppermute | solution.py:19
  18.0 1.4 %collective-permute-done.3 = f32[3,16,4,128]{3,2,1,0:T(4,128)S(1)} collective-permute-done((f32[3,16,4,128]{3,2,1,0:T(4,128)S(1)}, f32[3,16,4,128]{3,2,1,0:T(4,128)S(1)}, u32[]{:S(2)}, u32[]{:S(2)}) %collective-permute-start.3) | collective-permute-done | bytes 98336 | tf_op jit(solution)/shard_map/ppermute | solution.py:22
  19.4 0.1 pad_maximum_fusion.1
  19.6 0.3 fusion.105
  19.9 0.4 copy.18
  20.3 1.6 %collective-permute-start.4 = (f32[3,16,40,4]{2,1,3,0:T(8,128)S(1)}, f32[3,16,40,4]{2,1,3,0:T(8,128)S(1)}, u32[]{:S(2)}, u32[]{:S(2)}) collective-permute-start(f32[3,16,40,4]{2,1,3,0:T(8,128)S(1)} %copy.18), channel_id=1, source_target_pairs={{0,1},{1,0},{2,3},{3,2},{4,5},{5,4},{6,7},{7,6},{8,9},{9,8},{10,11... | collective-permute-start | bytes 92168 | tf_op jit(solution)/shard_map/ppermute | solution.py:19
  21.8 0.4 copy.19
  22.2 0.6 collective-permute-start.5
  22.8 0.1 fusion.55
  22.9 2.8 %collective-permute-done.4 = f32[3,16,40,4]{2,1,3,0:T(8,128)S(1)} collective-permute-done((f32[3,16,40,4]{2,1,3,0:T(8,128)S(1)}, f32[3,16,40,4]{2,1,3,0:T(8,128)S(1)}, u32[]{:S(2)}, u32[]{:S(2)}) %collective-permute-start.4) | collective-permute-done | bytes 30752 | tf_op jit(solution)/shard_map/ppermute | solution.py:19
  25.7 0.4 copy.20
  26.1 1.0 collective-permute-done.5
  27.1 0.4 copy.21
  27.5 1.1 pad_maximum_fusion
  28.6 0.2 slice_add_fusion.15
  28.8 0.2 slice_add_fusion.16
  29.0 0.2 slice_add_fusion.17
  29.2 1.9 %fusion.6 = f32[2,14,38,134]{3,2,1,0:T(8,128)S(1)} fusion(f32[3,16,40,136]{3,2,1,0:T(8,128)S(1)} %pad_maximum_fusion, f32[14,38,134]{2,1,0:T(8,128)S(1)} %slice_add_fusion.15), kind=kLoop, calls=%fused_computation.8 | loop fusion | flops 1425760 | bytes 4847584 | tf_op jit(solution)/shard_map/div | solution.py:43
  31.1 1.9 %slice_subtract_fusion = f32[2,12,36,132]{3,2,1,0:T(8,128)S(1)} fusion(f32[3,16,40,136]{3,2,1,0:T(8,128)S(1)} %pad_maximum_fusion, f32[2,14,38,134]{3,2,1,0:T(8,128)S(1)} %fusion.6, f32[12,36,132]{2,1,0:T(8,128)S(1)} %slice_add_fusion.16), kind=kLoop, calls=%fused_computation.43 | loop fusion | flops 1254528 | bytes 4333824 | tf_op jit(solution)/shard_map/sub | solution.py:46
  33.0 1.6 %slice_subtract_fusion.1 = f32[2,10,34,130]{3,2,1,0:T(8,128)S(1)} fusion(f32[2,14,38,134]{3,2,1,0:T(8,128)S(1)} %fusion.6, f32[2,12,36,132]{3,2,1,0:T(8,128)S(1)} %slice_subtract_fusion, f32[10,34,130]{2,1,0:T(8,128)S(1)} %slice_add_fusion.17), kind=kLoop, calls=%fused_computation.53 | loop fusion | flops 972400 | bytes 3359200 | tf_op jit(solution)/shard_map/sub | solution.py:46
  34.6 0.3 slice_subtract_fusion.2
  35.0 0.1 slice_bitcast_fusion.3
  35.1 0.1 slice_bitcast_fusion.1
  35.1 0.1 slice.279
  35.3 0.1 slice.294
  35.4 0.1 slice.268
  35.5 0.1 slice.292
  35.6 0.1 slice.290
  35.7 0.1 slice.257
  35.8 2.1 %stack.65 = f32[9,8,32,128]{3,0,2,1:T(8,128)S(1)} concatenate(f32[1,8,32,128]{3,0,2,1:T(1,128)S(1)} %bitcast.249, f32[1,8,32,128]{3,0,2,1:T(1,128)S(1)} %bitcast.273, f32[1,8,32,128]{3,0,2,1:T(1,128)S(1)} %bitcast.267, f32[1,8,32,128]{3,0,2,1:T(1,128)S(1)} %bitcast.263, f32[1,8,32,128]{3,0,2,1:T(1,128)S(1)} %bitcast.261, f32[1,8,32,128]{3,0,2,1:T(1,128)S(1)} %bitcast.255, ...), dimensions={0} | concatenate | bytes 2359296 | tf_op jit(solution)/shard_map/stack | solution.py:111
  37.8 2.9 %convolution_bitcast_fusion.1 = f32[9,9]{0,1:T(8,128)S(1)} fusion(f32[9,8,32,128]{3,0,2,1:T(8,128)S(1)} %stack.65), kind=kOutput, calls=%fused_computation.14 | convolution fusion | flops 31850496 | bytes 1179972 | tf_op jit(solution)/shard_map/dot_general | solution.py:113
  40.7 1.9 %stack.75 = f32[9,32768]{1,0:T(8,128)S(1)} concatenate(f32[1,32768]{1,0:T(1,128)S(1)} %bitcast.250, f32[1,32768]{1,0:T(1,128)S(1)} %bitcast.274, f32[1,32768]{1,0:T(1,128)S(1)} %bitcast.268, f32[1,32768]{1,0:T(1,128)S(1)} %bitcast.264, f32[1,32768]{1,0:T(1,128)S(1)} %bitcast.262, f32[1,32768]{1,0:T(1,128)S(1)} %bitcast.256, f32[1,32768]{1,0:T(1,128)S(1)} %bitcast.272, ...), dimensions={0} | concatenate | bytes 2359296 | tf_op jit(solution)/shard_map/stack | solution.py:111
  42.6 2.0 %convolution_bitcast_fusion = f32[16,9]{0,1:T(8,128)S(1)} fusion(bf16[2,8,256,128]{3,2,1,0:T(8,128)(2,1)} %bitcast.275, f32[9,32768]{1,0:T(8,128)S(1)} %stack.75), kind=kOutput, calls=%fused_computation.13 | convolution fusion | flops 9732096 | bytes 2228800 | tf_op jit(solution)/shard_map/dot_general | solution.py:122
  44.6 0.1 pad_maximum_fusion.8
  44.7 40.0 %psum.7 = f32[25,9]{0,1:T(8,128)S(1)} all-reduce(f32[25,9]{0,1:T(8,128)S(1)} %pad_maximum_fusion.8), channel_id=1, replica_groups=mesh['gx'=4,'gy'=4,'gz'=2] {'gx','gy','gz'}, use_global_device_ids=true, to_apply=%region_0.0 | all-reduce | flops 225 | bytes 1800 | tf_op jit(solution)/shard_map/psum | solution.py:125
  84.7 0.7 fusion.31
  85.4 0.7 fusion.30
  87.5 0.7 fusion.32
  89.6 0.1 fusion.89
  89.7 0.8 fusion.33
  91.8 0.7 fusion.34
  93.9 0.1 fusion.87
  94.0 0.8 fusion.35
  96.1 0.8 fusion.36
  98.3 0.1 fusion.85
  98.5 0.8 fusion.37
  100.6 0.2 convolution_bitcast_fusion.3
  100.8 0.7 fusion.38
  101.6 0.4 copy.55
  102.0 0.1 slice.297
  102.1 2.4 %fusion = f32[1,8,32,128]{3,0,2,1:T(1,128)} fusion(f32[8,32,128,9]{2,1,0,3:T(8,128)S(1)} %bitcast.242, f32[9]{0:T(128)S(1)} %fusion.67), kind=kOutput, calls=%fused_computation | convolution fusion | flops 3538944 | bytes 1310756 | tf_op jit(solution)/shard_map/dot_general | solution.py:129
  104.5 2.4 %fusion.2 = f32[1,8,32,128]{3,0,2,1:T(1,128)} fusion(f32[8,32,128,9]{2,1,0,3:T(8,128)S(1)} %bitcast.243, f32[9]{0:T(128)S(1)} %multiply_add_fusion, f32[9]{0:T(128)S(1)} %multiply_add_fusion.1, f32[9]{0:T(128)S(1)} %select_add_fusion, f32[]{:T(128)S(6)} %div.44, f32[]{:T(128)S(6)} %div.42, f32[]{:T(128)S(6)} %div.40, f32[]{:T(128)S(6)} %div.38), kind=kOutput, calls=%fused_computation.2 | convolution fusion | flops 3539016 | bytes 1310844 | tf_op jit(solution)/shard_map/dot_general | solution.py:128
  108.3 1.1 %fusion.62 = f32[1,32768]{1,0:T(1,128)S(1)} fusion(f32[9,32768]{1,0:T(8,128)S(1)} %stack.75, f32[9]{0:T(128)S(1)} %fusion.67, f32[9]{0:T(128)S(1)} %multiply_add_fusion, f32[]{:T(128)S(6)} %div.45), kind=kOutput, calls=%fused_computation.119 | convolution fusion | flops 3538962 | bytes 1310796 | tf_op jit(solution)/shard_map/dot_general | solution.py:133
  109.4 0.1 fusion.15
  109.5 0.7 fusion.18
  110.2 0.7 sub.63
  (21 shorter events, 0.2 us)
Async XLA Ops:
  0.6 108.8 %copy-start = (f32[16,16]{1,0:T(8,128)S(1)}, f32[16,16]{1,0:T(8,128)}, u32[]{:S(2)}) copy-start(f32[16,16]{1,0:T(8,128)} %param.12) | copy-start | bytes 3076
  0.6 18.8 %copy-start.1 = (f32[8,32,128]{2,1,0:T(8,128)S(1)}, f32[8,32,128]{2,1,0:T(8,128)}, u32[]{:S(2)}) copy-start(f32[8,32,128]{2,1,0:T(8,128)} %param.8) | copy-start | bytes 393220
  0.7 18.8 %copy-start.2 = (f32[8,32,128]{2,1,0:T(8,128)S(1)}, f32[8,32,128]{2,1,0:T(8,128)}, u32[]{:S(2)}) copy-start(f32[8,32,128]{2,1,0:T(8,128)} %param.7) | copy-start | bytes 393220
  0.7 18.8 %copy-start.3 = (f32[8,32,128]{2,1,0:T(8,128)S(1)}, f32[8,32,128]{2,1,0:T(8,128)}, u32[]{:S(2)}) copy-start(f32[8,32,128]{2,1,0:T(8,128)} %param.9) | copy-start | bytes 393220
  1.8 5.8 %collective-permute-start = (f32[3,4,32,128]{3,2,1,0:T(8,128)S(1)}, f32[3,4,32,128]{3,2,1,0:T(8,128)S(1)}, u32[]{:S(2)}, u32[]{:S(2)}) collective-permute-start(f32[3,4,32,128]{3,2,1,0:T(8,128)S(1)} %get-tuple-element.13), channel_id=1, source_target_pairs={{0,8},{8,16},{16,24},{24,0},{1,9},{9,17},{17,25},{25,1},{2,10},{10... | collective-permute-start | bytes 589832 | tf_op jit(solution)/shard_map/ppermute | solution.py:19
  2.4 7.2 %collective-permute-start.1 = (f32[3,4,32,128]{3,2,1,0:T(8,128)S(1)}, f32[3,4,32,128]{3,2,1,0:T(8,128)S(1)}, u32[]{:S(2)}, u32[]{:S(2)}) collective-permute-start(f32[3,4,32,128]{3,2,1,0:T(8,128)S(1)} %get-tuple-element.14), channel_id=1, source_target_pairs={{8,0},{16,8},{24,16},{0,24},{9,1},{17,9},{25,17},{1,25},{10,2},{18... | collective-permute-start | bytes 589832 | tf_op jit(solution)/shard_map/ppermute | solution.py:22
  10.5 7.5 %collective-permute-start.2 = (f32[3,16,4,128]{3,2,1,0:T(4,128)S(1)}, f32[3,16,4,128]{3,2,1,0:T(4,128)S(1)}, u32[]{:S(2)}, u32[]{:S(2)}) collective-permute-start(f32[3,16,4,128]{3,2,1,0:T(4,128)S(1)} %get-tuple-element.11), channel_id=1, source_target_pairs={{0,2},{2,4},{4,6},{6,0},{1,3},{3,5},{5,7},{7,1},{8,10},{10,12},{12... | collective-permute-start | bytes 294920 | tf_op jit(solution)/shard_map/ppermute | solution.py:19
  12.1 7.3 %collective-permute-start.3 = (f32[3,16,4,128]{3,2,1,0:T(4,128)S(1)}, f32[3,16,4,128]{3,2,1,0:T(4,128)S(1)}, u32[]{:S(2)}, u32[]{:S(2)}) collective-permute-start(f32[3,16,4,128]{3,2,1,0:T(4,128)S(1)} %get-tuple-element.12), channel_id=1, source_target_pairs={{2,0},{4,2},{6,4},{0,6},{3,1},{5,3},{7,5},{1,7},{10,8},{12,10},{14... | collective-permute-start | bytes 294920 | tf_op jit(solution)/shard_map/ppermute | solution.py:22
  19.9 2.9 %copy-start.5 = (f32[9,9]{1,0:T(8,128)S(1)}, f32[9,9]{1,0:T(8,128)}, u32[]{:S(2)}) copy-start(f32[9,9]{1,0:T(8,128)} %constant.17.clone) | copy-start | bytes 976
  20.3 5.4 %collective-permute-start.4 = (f32[3,16,40,4]{2,1,3,0:T(8,128)S(1)}, f32[3,16,40,4]{2,1,3,0:T(8,128)S(1)}, u32[]{:S(2)}, u32[]{:S(2)}) collective-permute-start(f32[3,16,40,4]{2,1,3,0:T(8,128)S(1)} %copy.18), channel_id=1, source_target_pairs={{0,1},{1,0},{2,3},{3,2},{4,5},{5,4},{6,7},{7,6},{8,9},{9,8},{10,11... | collective-permute-start | bytes 92168 | tf_op jit(solution)/shard_map/ppermute | solution.py:19
  22.2 4.9 %collective-permute-start.5 = (f32[3,16,40,4]{2,1,3,0:T(8,128)S(1)}, f32[3,16,40,4]{2,1,3,0:T(8,128)S(1)}, u32[]{:S(2)}, u32[]{:S(2)}) collective-permute-start(f32[3,16,40,4]{2,1,3,0:T(8,128)S(1)} %copy.19), channel_id=1, source_target_pairs={{1,0},{0,1},{3,2},{2,3},{5,4},{4,5},{7,6},{6,7},{9,8},{8,9},{11,10... | collective-permute-start | bytes 92168 | tf_op jit(solution)/shard_map/ppermute | solution.py:22
  104.5 5.1 %copy-start.4 = (bf16[16,8,32,128]{3,2,1,0:T(8,128)(2,1)S(1)}, bf16[16,8,32,128]{3,2,1,0:T(8,128)(2,1)}, u32[]{:S(2)}) copy-start(bf16[16,8,32,128]{3,2,1,0:T(8,128)(2,1)} %param.10) | copy-start | bytes 3145732
where the time goes:
time: 111 us
  blocking collectives  40 us (36%)
  matrix products  19.1 us (17%)
  waiting for transfers between devices  14 us (13%)
  between operations  11.8 us (11%)
  other arithmetic  10.2 us (9%)
  starting transfers between devices  8.58 us (8%)
  local copies, waits for them, and re-layouts  7.23 us (7%)
    psum x1, blocking collectives, body(): lax.psum(jnp.concatenate([gram_block, projections], 0), ('gx', 'gy', 'gz'))  40 us
    ppermute x3, waiting for transfers between devices, extended(): lax.ppermute(lax.slice_in_dim(block, block.shape[dim] - width, None, axis...  9.69 us
    ppermute x3, starting transfers between devices, extended(): lax.ppermute(lax.slice_in_dim(block, 0, width, axis=dim), axis, backward)  4.85 us
    ppermute x3, waiting for transfers between devices, extended(): lax.ppermute(lax.slice_in_dim(block, 0, width, axis=dim), axis, backward)  4.3 us
    another operation x2, local copies, waits for them, and re-layouts, body(): basis = jnp.stack(search_basis + residue_basis)  3.93 us
    sub x3, other arithmetic, chebyshev_next(): return 2.0 * scaled - earlier  3.83 us
    dot_general x5, matrix products, coordinates(): jnp.dot(gram_block, residue, precision=precise)  3.78 us
    ppermute x3, starting transfers between devices, extended(): lax.ppermute(lax.slice_in_dim(block, block.shape[dim] - width, None, axis...  3.73 us
  transfers between devices with their start and end apart: 6, of which 6 were waited for; matrix products, arithmetic and copies ran while one was open for 1% of the time, Pallas kernels for 0%

commit v1 on v0

--- a/solution.py
+++ b/solution.py
@@ -122,7 +122,9 @@
     projections = lax.dot_general(
         images, rounded, (((1,), (1,)), ((), ())), preferred_element_type=jnp.float32
     )
-    totals = lax.psum(jnp.concatenate([gram_block, projections], 0), ("gx", "gy", "gz"))
+    totals = jnp.sum(
+        lax.all_gather(jnp.concatenate([gram_block, projections], 0), ("gx", "gy", "gz")), axis=0
+    )
     update, residue, search, weights = coordinates(totals, coupling_inverse)
     shape = residual.shape
     solution_delta = jnp.dot(update, basis_flat, precision=precise).reshape(shape)

time: 111 us -> 138 us (1.24)
  blocking collectives: 40 us -> 66.7 us
    all_gather x0 -> x1, blocking collectives: none -> 66.7 us  [body(): lax.all_gather(jnp.concatenate([gram_block, projections], 0), ('gx', 'gy'...]
    psum x1 -> x0, blocking collectives: 40 us -> none  [body(): lax.psum(jnp.concatenate([gram_block, projections], 0), ('gx', 'gy', 'gz'))]
where the time goes in v1:
time: 138 us
  blocking collectives  66.7 us (48%)
  matrix products  19.1 us (14%)
  waiting for transfers between devices  14 us (10%)
  between operations  11.8 us (9%)
  other arithmetic  10.3 us (7%)
  starting transfers between devices  8.58 us (6%)
  local copies, waits for them, and re-layouts  7.23 us (5%)
    all_gather x1, blocking collectives, body(): lax.all_gather(jnp.concatenate([gram_block, projections], 0), ('gx', 'gy'...  66.7 us
    ppermute x3, waiting for transfers between devices, extended(): lax.ppermute(lax.slice_in_dim(block, block.shape[dim] - width, None, axis...  9.69 us
    ppermute x3, starting transfers between devices, extended(): lax.ppermute(lax.slice_in_dim(block, 0, width, axis=dim), axis, backward)  4.85 us
    ppermute x3, waiting for transfers between devices, extended(): lax.ppermute(lax.slice_in_dim(block, 0, width, axis=dim), axis, backward)  4.3 us
    another operation x2, local copies, waits for them, and re-layouts, body(): basis = jnp.stack(search_basis + residue_basis)  3.93 us
    sub x3, other arithmetic, chebyshev_next(): return 2.0 * scaled - earlier  3.83 us
    dot_general x5, matrix products, coordinates(): jnp.dot(gram_block, residue, precision=precise)  3.78 us
    ppermute x3, starting transfers between devices, extended(): lax.ppermute(lax.slice_in_dim(block, block.shape[dim] - width, None, axis...  3.73 us
  transfers between devices with their start and end apart: 6, of which 6 were waited for; matrix products, arithmetic and copies ran while one was open for 1% of the time, Pallas kernels for 0%

profile of v1, /device:TPU:0, one launch (start us, length us, event | category | flops | bytes accessed | tf_op | source)
XLA Modules:
  0.0 137.6 jit_solution(17090647900251413648)
XLA Ops:
  0.7 1.1 pad_maximum_fusion.2
  1.8 0.5 collective-permute-start
  2.4 2.0 %collective-permute-start.1 = (f32[3,4,32,128]{3,2,1,0:T(8,128)S(1)}, f32[3,4,32,128]{3,2,1,0:T(8,128)S(1)}, u32[]{:S(2)}, u32[]{:S(2)}) collective-permute-start(f32[3,4,32,128]{3,2,1,0:T(8,128)S(1)} %get-tuple-element.14), channel_id=1, source_target_pairs={{8,0},{16,8},{24,16},{0,24},{9,1},{17,9},{25,17},{1,25},{10,2},{18... | collective-permute-start | bytes 589832 | tf_op jit(solution)/shard_map/ppermute | solution.py:22
  4.4 3.3 %collective-permute-done = f32[3,4,32,128]{3,2,1,0:T(8,128)S(1)} collective-permute-done((f32[3,4,32,128]{3,2,1,0:T(8,128)S(1)}, f32[3,4,32,128]{3,2,1,0:T(8,128)S(1)}, u32[]{:S(2)}, u32[]{:S(2)}) %collective-permute-start) | collective-permute-done | bytes 196640 | tf_op jit(solution)/shard_map/ppermute | solution.py:19
  7.7 1.9 %collective-permute-done.1 = f32[3,4,32,128]{3,2,1,0:T(8,128)S(1)} collective-permute-done((f32[3,4,32,128]{3,2,1,0:T(8,128)S(1)}, f32[3,4,32,128]{3,2,1,0:T(8,128)S(1)}, u32[]{:S(2)}, u32[]{:S(2)}) %collective-permute-start.1) | collective-permute-done | bytes 196640 | tf_op jit(solution)/shard_map/ppermute | solution.py:22
  9.6 0.9 pad_maximum_fusion.7
  10.5 1.6 %collective-permute-start.2 = (f32[3,16,4,128]{3,2,1,0:T(4,128)S(1)}, f32[3,16,4,128]{3,2,1,0:T(4,128)S(1)}, u32[]{:S(2)}, u32[]{:S(2)}) collective-permute-start(f32[3,16,4,128]{3,2,1,0:T(4,128)S(1)} %get-tuple-element.11), channel_id=1, source_target_pairs={{0,2},{2,4},{4,6},{6,0},{1,3},{3,5},{5,7},{7,1},{8,10},{10,12},{12... | collective-permute-start | bytes 294920 | tf_op jit(solution)/shard_map/ppermute | solution.py:19
  12.1 2.2 %collective-permute-start.3 = (f32[3,16,4,128]{3,2,1,0:T(4,128)S(1)}, f32[3,16,4,128]{3,2,1,0:T(4,128)S(1)}, u32[]{:S(2)}, u32[]{:S(2)}) collective-permute-start(f32[3,16,4,128]{3,2,1,0:T(4,128)S(1)} %get-tuple-element.12), channel_id=1, source_target_pairs={{2,0},{4,2},{6,4},{0,6},{3,1},{5,3},{7,5},{1,7},{10,8},{12,10},{14... | collective-permute-start | bytes 294920 | tf_op jit(solution)/shard_map/ppermute | solution.py:22
  14.4 3.7 %collective-permute-done.2 = f32[3,16,4,128]{3,2,1,0:T(4,128)S(1)} collective-permute-done((f32[3,16,4,128]{3,2,1,0:T(4,128)S(1)}, f32[3,16,4,128]{3,2,1,0:T(4,128)S(1)}, u32[]{:S(2)}, u32[]{:S(2)}) %collective-permute-start.2) | collective-permute-done | bytes 98336 | tf_op jit(solution)/shard_map/ppermute | solution.py:19
  18.0 1.4 %collective-permute-done.3 = f32[3,16,4,128]{3,2,1,0:T(4,128)S(1)} collective-permute-done((f32[3,16,4,128]{3,2,1,0:T(4,128)S(1)}, f32[3,16,4,128]{3,2,1,0:T(4,128)S(1)}, u32[]{:S(2)}, u32[]{:S(2)}) %collective-permute-start.3) | collective-permute-done | bytes 98336 | tf_op jit(solution)/shard_map/ppermute | solution.py:22
  19.4 0.1 pad_maximum_fusion.1
  19.6 0.3 fusion.105
  19.9 0.4 copy.18
  20.3 1.6 %collective-permute-start.4 = (f32[3,16,40,4]{2,1,3,0:T(8,128)S(1)}, f32[3,16,40,4]{2,1,3,0:T(8,128)S(1)}, u32[]{:S(2)}, u32[]{:S(2)}) collective-permute-start(f32[3,16,40,4]{2,1,3,0:T(8,128)S(1)} %copy.18), channel_id=1, source_target_pairs={{0,1},{1,0},{2,3},{3,2},{4,5},{5,4},{6,7},{7,6},{8,9},{9,8},{10,11... | collective-permute-start | bytes 92168 | tf_op jit(solution)/shard_map/ppermute | solution.py:19
  21.8 0.4 copy.19
  22.2 0.6 collective-permute-start.5
  22.8 0.1 fusion.55
  22.9 2.8 %collective-permute-done.4 = f32[3,16,40,4]{2,1,3,0:T(8,128)S(1)} collective-permute-done((f32[3,16,40,4]{2,1,3,0:T(8,128)S(1)}, f32[3,16,40,4]{2,1,3,0:T(8,128)S(1)}, u32[]{:S(2)}, u32[]{:S(2)}) %collective-permute-start.4) | collective-permute-done | bytes 30752 | tf_op jit(solution)/shard_map/ppermute | solution.py:19
  25.7 0.4 copy.20
  26.1 1.0 collective-permute-done.5
  27.1 0.4 copy.21
  27.5 1.1 pad_maximum_fusion
  28.6 0.2 slice_add_fusion.15
  28.8 0.2 slice_add_fusion.16
  29.0 0.2 slice_add_fusion.17
  29.2 1.9 %fusion.6 = f32[2,14,38,134]{3,2,1,0:T(8,128)S(1)} fusion(f32[3,16,40,136]{3,2,1,0:T(8,128)S(1)} %pad_maximum_fusion, f32[14,38,134]{2,1,0:T(8,128)S(1)} %slice_add_fusion.15), kind=kLoop, calls=%fused_computation.8 | loop fusion | flops 1425760 | bytes 4847584 | tf_op jit(solution)/shard_map/div | solution.py:43
  31.1 1.9 %slice_subtract_fusion = f32[2,12,36,132]{3,2,1,0:T(8,128)S(1)} fusion(f32[3,16,40,136]{3,2,1,0:T(8,128)S(1)} %pad_maximum_fusion, f32[2,14,38,134]{3,2,1,0:T(8,128)S(1)} %fusion.6, f32[12,36,132]{2,1,0:T(8,128)S(1)} %slice_add_fusion.16), kind=kLoop, calls=%fused_computation.43 | loop fusion | flops 1254528 | bytes 4333824 | tf_op jit(solution)/shard_map/sub | solution.py:46
  33.0 1.6 %slice_subtract_fusion.1 = f32[2,10,34,130]{3,2,1,0:T(8,128)S(1)} fusion(f32[2,14,38,134]{3,2,1,0:T(8,128)S(1)} %fusion.6, f32[2,12,36,132]{3,2,1,0:T(8,128)S(1)} %slice_subtract_fusion, f32[10,34,130]{2,1,0:T(8,128)S(1)} %slice_add_fusion.17), kind=kLoop, calls=%fused_computation.53 | loop fusion | flops 972400 | bytes 3359200 | tf_op jit(solution)/shard_map/sub | solution.py:46
  34.6 0.3 slice_subtract_fusion.2
  35.0 0.1 slice_bitcast_fusion.3
  35.1 0.1 slice_bitcast_fusion.1
  35.1 0.1 slice.279
  35.3 0.1 slice.294
  35.4 0.1 slice.268
  35.5 0.1 slice.292
  35.6 0.1 slice.290
  35.7 0.1 slice.257
  35.8 2.1 %stack.65 = f32[9,8,32,128]{3,0,2,1:T(8,128)S(1)} concatenate(f32[1,8,32,128]{3,0,2,1:T(1,128)S(1)} %bitcast.251, f32[1,8,32,128]{3,0,2,1:T(1,128)S(1)} %bitcast.275, f32[1,8,32,128]{3,0,2,1:T(1,128)S(1)} %bitcast.269, f32[1,8,32,128]{3,0,2,1:T(1,128)S(1)} %bitcast.265, f32[1,8,32,128]{3,0,2,1:T(1,128)S(1)} %bitcast.263, f32[1,8,32,128]{3,0,2,1:T(1,128)S(1)} %bitcast.257, ...), dimensions={0} | concatenate | bytes 2359296 | tf_op jit(solution)/shard_map/stack | solution.py:111
  37.8 2.9 %convolution_bitcast_fusion.1 = f32[9,9]{0,1:T(8,128)S(1)} fusion(f32[9,8,32,128]{3,0,2,1:T(8,128)S(1)} %stack.65), kind=kOutput, calls=%fused_computation.14 | convolution fusion | flops 31850496 | bytes 1179972 | tf_op jit(solution)/shard_map/dot_general | solution.py:113
  40.7 1.9 %stack.75 = f32[9,32768]{1,0:T(8,128)S(1)} concatenate(f32[1,32768]{1,0:T(1,128)S(1)} %bitcast.252, f32[1,32768]{1,0:T(1,128)S(1)} %bitcast.276, f32[1,32768]{1,0:T(1,128)S(1)} %bitcast.270, f32[1,32768]{1,0:T(1,128)S(1)} %bitcast.266, f32[1,32768]{1,0:T(1,128)S(1)} %bitcast.264, f32[1,32768]{1,0:T(1,128)S(1)} %bitcast.258, f32[1,32768]{1,0:T(1,128)S(1)} %bitcast.274, ...), dimensions={0} | concatenate | bytes 2359296 | tf_op jit(solution)/shard_map/stack | solution.py:111
  42.6 2.0 %convolution_bitcast_fusion = f32[16,9]{0,1:T(8,128)S(1)} fusion(bf16[2,8,256,128]{3,2,1,0:T(8,128)(2,1)} %bitcast.277, f32[9,32768]{1,0:T(8,128)S(1)} %stack.75), kind=kOutput, calls=%fused_computation.13 | convolution fusion | flops 9732096 | bytes 2228800 | tf_op jit(solution)/shard_map/dot_general | solution.py:122
  44.6 0.1 maximum_bitcast_fusion
  44.7 66.7 %all-gather.1 = f32[32,25,9]{1,2,0:T(8,128)S(1)} all-gather(f32[1,25,9]{1,2,0:T(8,128)S(1)} %maximum_bitcast_fusion), channel_id=2, replica_groups=mesh['gx'=4,'gy'=4,'gz'=2] {'gx','gy','gz'}, dimensions={0}, use_global_device_ids=true | all-gather | bytes 29700 | tf_op jit(solution)/shard_map/all_gather | solution.py:126
  111.4 0.7 fusion.31
  112.1 0.7 fusion.30
  114.2 0.7 fusion.32
  116.3 0.1 fusion.89
  116.4 0.8 fusion.33
  118.5 0.7 fusion.34
  120.6 0.1 fusion.87
  120.7 0.8 fusion.35
  122.9 0.8 fusion.36
  125.1 0.1 fusion.85
  125.2 0.8 fusion.37
  127.3 0.2 convolution_bitcast_fusion.3
  127.5 0.7 fusion.38
  128.3 0.4 copy.55
  128.7 0.1 slice.297
  128.8 2.4 %fusion = f32[1,8,32,128]{3,0,2,1:T(1,128)} fusion(f32[8,32,128,9]{2,1,0,3:T(8,128)S(1)} %bitcast.244, f32[9]{0:T(128)S(1)} %fusion.67), kind=kOutput, calls=%fused_computation | convolution fusion | flops 3538944 | bytes 1310756 | tf_op jit(solution)/shard_map/dot_general | solution.py:131
  131.2 2.4 %fusion.2 = f32[1,8,32,128]{3,0,2,1:T(1,128)} fusion(f32[8,32,128,9]{2,1,0,3:T(8,128)S(1)} %bitcast.245, f32[9]{0:T(128)S(1)} %multiply_add_fusion, f32[9]{0:T(128)S(1)} %multiply_add_fusion.1, f32[9]{0:T(128)S(1)} %select_add_fusion, f32[]{:T(128)S(6)} %div.44, f32[]{:T(128)S(6)} %div.42, f32[]{:T(128)S(6)} %div.40, f32[]{:T(128)S(6)} %div.38), kind=kOutput, calls=%fused_computation.2 | convolution fusion | flops 3539016 | bytes 1310844 | tf_op jit(solution)/shard_map/dot_general | solution.py:130
  135.0 1.1 fusion.62
  136.1 0.1 fusion.15
  136.3 0.7 fusion.18
  136.9 0.7 sub.63
  (22 shorter events, 0.2 us)
Async XLA Ops:
  0.6 135.5 %copy-start = (f32[16,16]{1,0:T(8,128)S(1)}, f32[16,16]{1,0:T(8,128)}, u32[]{:S(2)}) copy-start(f32[16,16]{1,0:T(8,128)} %param.12) | copy-start | bytes 3076
  0.6 18.8 %copy-start.1 = (f32[8,32,128]{2,1,0:T(8,128)S(1)}, f32[8,32,128]{2,1,0:T(8,128)}, u32[]{:S(2)}) copy-start(f32[8,32,128]{2,1,0:T(8,128)} %param.8) | copy-start | bytes 393220
  0.7 18.8 %copy-start.2 = (f32[8,32,128]{2,1,0:T(8,128)S(1)}, f32[8,32,128]{2,1,0:T(8,128)}, u32[]{:S(2)}) copy-start(f32[8,32,128]{2,1,0:T(8,128)} %param.7) | copy-start | bytes 393220
  0.7 18.8 %copy-start.3 = (f32[8,32,128]{2,1,0:T(8,128)S(1)}, f32[8,32,128]{2,1,0:T(8,128)}, u32[]{:S(2)}) copy-start(f32[8,32,128]{2,1,0:T(8,128)} %param.9) | copy-start | bytes 393220
  1.8 5.8 %collective-permute-start = (f32[3,4,32,128]{3,2,1,0:T(8,128)S(1)}, f32[3,4,32,128]{3,2,1,0:T(8,128)S(1)}, u32[]{:S(2)}, u32[]{:S(2)}) collective-permute-start(f32[3,4,32,128]{3,2,1,0:T(8,128)S(1)} %get-tuple-element.13), channel_id=1, source_target_pairs={{0,8},{8,16},{16,24},{24,0},{1,9},{9,17},{17,25},{25,1},{2,10},{10... | collective-permute-start | bytes 589832 | tf_op jit(solution)/shard_map/ppermute | solution.py:19
  2.4 7.2 %collective-permute-start.1 = (f32[3,4,32,128]{3,2,1,0:T(8,128)S(1)}, f32[3,4,32,128]{3,2,1,0:T(8,128)S(1)}, u32[]{:S(2)}, u32[]{:S(2)}) collective-permute-start(f32[3,4,32,128]{3,2,1,0:T(8,128)S(1)} %get-tuple-element.14), channel_id=1, source_target_pairs={{8,0},{16,8},{24,16},{0,24},{9,1},{17,9},{25,17},{1,25},{10,2},{18... | collective-permute-start | bytes 589832 | tf_op jit(solution)/shard_map/ppermute | solution.py:22
  10.5 7.5 %collective-permute-start.2 = (f32[3,16,4,128]{3,2,1,0:T(4,128)S(1)}, f32[3,16,4,128]{3,2,1,0:T(4,128)S(1)}, u32[]{:S(2)}, u32[]{:S(2)}) collective-permute-start(f32[3,16,4,128]{3,2,1,0:T(4,128)S(1)} %get-tuple-element.11), channel_id=1, source_target_pairs={{0,2},{2,4},{4,6},{6,0},{1,3},{3,5},{5,7},{7,1},{8,10},{10,12},{12... | collective-permute-start | bytes 294920 | tf_op jit(solution)/shard_map/ppermute | solution.py:19
  12.1 7.3 %collective-permute-start.3 = (f32[3,16,4,128]{3,2,1,0:T(4,128)S(1)}, f32[3,16,4,128]{3,2,1,0:T(4,128)S(1)}, u32[]{:S(2)}, u32[]{:S(2)}) collective-permute-start(f32[3,16,4,128]{3,2,1,0:T(4,128)S(1)} %get-tuple-element.12), channel_id=1, source_target_pairs={{2,0},{4,2},{6,4},{0,6},{3,1},{5,3},{7,5},{1,7},{10,8},{12,10},{14... | collective-permute-start | bytes 294920 | tf_op jit(solution)/shard_map/ppermute | solution.py:22
  19.9 2.9 %copy-start.5 = (f32[9,9]{1,0:T(8,128)S(1)}, f32[9,9]{1,0:T(8,128)}, u32[]{:S(2)}) copy-start(f32[9,9]{1,0:T(8,128)} %constant.17.clone) | copy-start | bytes 976
  20.3 5.4 %collective-permute-start.4 = (f32[3,16,40,4]{2,1,3,0:T(8,128)S(1)}, f32[3,16,40,4]{2,1,3,0:T(8,128)S(1)}, u32[]{:S(2)}, u32[]{:S(2)}) collective-permute-start(f32[3,16,40,4]{2,1,3,0:T(8,128)S(1)} %copy.18), channel_id=1, source_target_pairs={{0,1},{1,0},{2,3},{3,2},{4,5},{5,4},{6,7},{7,6},{8,9},{9,8},{10,11... | collective-permute-start | bytes 92168 | tf_op jit(solution)/shard_map/ppermute | solution.py:19
  22.2 4.9 %collective-permute-start.5 = (f32[3,16,40,4]{2,1,3,0:T(8,128)S(1)}, f32[3,16,40,4]{2,1,3,0:T(8,128)S(1)}, u32[]{:S(2)}, u32[]{:S(2)}) collective-permute-start(f32[3,16,40,4]{2,1,3,0:T(8,128)S(1)} %copy.19), channel_id=1, source_target_pairs={{1,0},{0,1},{3,2},{2,3},{5,4},{4,5},{7,6},{6,7},{9,8},{8,9},{11,10... | collective-permute-start | bytes 92168 | tf_op jit(solution)/shard_map/ppermute | solution.py:22
  131.2 5.1 %copy-start.4 = (bf16[16,8,32,128]{3,2,1,0:T(8,128)(2,1)S(1)}, bf16[16,8,32,128]{3,2,1,0:T(8,128)(2,1)}, u32[]{:S(2)}) copy-start(bf16[16,8,32,128]{3,2,1,0:T(8,128)(2,1)} %param.10) | copy-start | bytes 3145732
